TPU v7x, 32 devices: a whole 2x2x4 slice. The times are simulated.
32 devices in a mesh: dp: 8 (over z, y), mp: 2 (over core), fsdp: 2 (over x).
Axes of the slice: x: 2, y: 2, z: 4, core: 2. Of those that a mesh axis runs over, the one named last changes fastest.
Arguments:
- features: bfloat16 [5, 1024, 512], P(None, ('dp', 'fsdp')), may hold values from -6 to 6
- memory_bank: bfloat16 [512, 32, 1024], P(('dp', 'fsdp')), may hold values from -1 to 1
- memory_fill: int32 [512], P(('dp', 'fsdp')), may hold values from 0 to 32
- left_keys: bfloat16 [512, 64, 1024], P(('dp', 'fsdp'), None, 'mp'), may hold values from -400 to 400
- left_values: bfloat16 [512, 64, 1024], P(('dp', 'fsdp'), None, 'mp'), may hold values from -6 to 6
- left_length: int32 [512], P(('dp', 'fsdp')), may hold values from 0 to 64
- w_query: bfloat16 [1024, 1024], P('fsdp', 'mp'), may hold values from -0.1875 to 0.1875
- w_key: bfloat16 [1024, 1024], P('fsdp', 'mp'), may hold values from -0.1875 to 0.1875
- w_value: bfloat16 [1024, 1024], P('fsdp', 'mp'), may hold values from -0.1875 to 0.1875
- w_out: bfloat16 [1024, 1024], P('mp', 'fsdp'), may hold values from -0.1875 to 0.1875
- w_up: bfloat16 [1024, 4096], P('fsdp', 'mp'), may hold values from -0.1875 to 0.1875
- w_down: bfloat16 [4096, 1024], P('mp', 'fsdp'), may hold values from -0.09375 to 0.09375
- out_gain: float32 [1024], replicated, may hold values from 0.1 to 1.9
Outputs:
- layer_out: bfloat16 [512, 5, 1024], P(('dp', 'fsdp'))
- memory_next: bfloat16 [512, 1024], P(('dp', 'fsdp'))
- center_keys: bfloat16 [512, 4, 1024], P(('dp', 'fsdp'), None, 'mp')
- center_values: bfloat16 [512, 4, 1024], P(('dp', 'fsdp'), None, 'mp')
All inputs are finite; a program needn't handle non-finite values.
Results may differ from a plain program's by a relative error of at most 0.0095.
Values may be sent and summed in bfloat16 or wider, within the bound.
A program may use at most 128 MiB of HBM per device.

v0:
```python
import jax
import jax.numpy as jnp
from jax import lax
from jax.sharding import PartitionSpec as P

HD = 64
GROUP = 4
epsilon = 1e-05
masked_score = -1e30


def normalize(values):
    values = values.astype(jnp.float32)
    average = jnp.mean(values, axis=-1, keepdims=True)
    centred = values - average
    variance = jnp.mean(centred * centred, axis=-1, keepdims=True)
    return centred * lax.rsqrt(variance + epsilon)


def matmul(left, right):
    return jnp.dot(left, right, preferred_element_type=jnp.float32)


def shards(
    features,
    memory_bank,
    memory_fill,
    left_keys,
    left_values,
    left_length,
    w_query,
    w_key,
    w_value,
    w_out,
    w_up,
    w_down,
    out_gain,
):
    frames, width_dev, all_streams = features.shape
    streams, mem_slots, width = memory_bank.shape
    left_slots = left_keys.shape[1]
    head_cols = w_query.shape[1]
    head_count = head_cols // HD
    flattened = features.reshape(frames * width_dev, all_streams)
    n_dp = lax.axis_size("dp")
    n_fsdp = lax.axis_size("fsdp")
    arrived = lax.all_to_all(flattened, ("dp", "fsdp"), split_axis=1, concat_axis=0, tiled=True)
    arrived = arrived.reshape(n_dp * n_fsdp, frames, width_dev, streams)
    inputs = jnp.transpose(arrived, (3, 1, 0, 2)).reshape(streams, frames, width)
    normed = normalize(inputs).astype(jnp.bfloat16)
    summary = jnp.mean(normed[:, :GROUP, :].astype(jnp.float32), axis=1).astype(jnp.bfloat16)
    query_rows = jnp.concatenate([normed, summary[:, None, :]], axis=1).reshape(-1, width)
    key_rows = jnp.concatenate([normed.reshape(-1, width), memory_bank.reshape(-1, width)], axis=0)
    query_sums = matmul(query_rows, lax.all_gather(w_query, "fsdp", axis=0, tiled=True))
    key_sums = matmul(key_rows, lax.all_gather(w_key, "fsdp", axis=0, tiled=True))
    value_sums = matmul(key_rows, lax.all_gather(w_value, "fsdp", axis=0, tiled=True))
    query_proj = query_sums.astype(jnp.bfloat16)
    key_proj = key_sums.astype(jnp.bfloat16)
    value_proj = value_sums.astype(jnp.bfloat16)
    group_total = streams * frames
    query_h = query_proj.reshape(streams, frames + 1, head_count, HD)
    ckey_h = key_proj[:group_total].reshape(streams, frames, head_count, HD)
    cval_h = value_proj[:group_total].reshape(streams, frames, head_count, HD)
    mkey_h = key_proj[group_total:].reshape(streams, mem_slots, head_count, HD)
    mval_h = value_proj[group_total:].reshape(streams, mem_slots, head_count, HD)
    lkey_h = left_keys.reshape(streams, left_slots, head_count, HD)
    lval_h = left_values.reshape(streams, left_slots, head_count, HD)
    not_summary = jnp.arange(frames + 1, dtype=jnp.int32) < frames
    mem_ok = jnp.arange(mem_slots, dtype=jnp.int32)[None, :] >= (mem_slots - memory_fill)[:, None]
    mem_mask = mem_ok[:, None, None, :] & not_summary[None, None, :, None]
    left_ok = (
        jnp.arange(left_slots, dtype=jnp.int32)[None, :] >= (left_slots - left_length)[:, None]
    )
    left_mask = left_ok[:, None, None, :]
    scale = HD ** (-0.5)
    score_mem = (
        jnp.einsum("sqhd,skhd->shqk", query_h, mkey_h, preferred_element_type=jnp.float32) * scale
    )
    score_left = (
        jnp.einsum("sqhd,skhd->shqk", query_h, lkey_h, preferred_element_type=jnp.float32) * scale
    )
    score_group = (
        jnp.einsum("sqhd,skhd->shqk", query_h, ckey_h, preferred_element_type=jnp.float32) * scale
    )
    score_mem = jnp.where(mem_mask, score_mem, masked_score)
    score_left = jnp.where(left_mask, score_left, masked_score)
    top = jnp.maximum(
        jnp.maximum(
            jnp.max(score_mem, axis=-1, keepdims=True), jnp.max(score_left, axis=-1, keepdims=True)
        ),
        jnp.max(score_group, axis=-1, keepdims=True),
    )
    exp_mem = jnp.exp(score_mem - top)
    exp_left = jnp.exp(score_left - top)
    exp_group = jnp.exp(score_group - top)
    totals = (
        jnp.sum(exp_mem, axis=-1, keepdims=True)
        + jnp.sum(exp_left, axis=-1, keepdims=True)
        + jnp.sum(exp_group, axis=-1, keepdims=True)
    )
    prob_mem = (exp_mem / totals).astype(jnp.bfloat16)
    prob_left = (exp_left / totals).astype(jnp.bfloat16)
    prob_group = (exp_group / totals).astype(jnp.bfloat16)
    attended = jnp.einsum("shqk,skhd->sqhd", prob_mem, mval_h, preferred_element_type=jnp.float32)
    attended = attended + jnp.einsum(
        "shqk,skhd->sqhd", prob_left, lval_h, preferred_element_type=jnp.float32
    )
    attended = attended + jnp.einsum(
        "shqk,skhd->sqhd", prob_group, cval_h, preferred_element_type=jnp.float32
    )
    attended = attended.astype(jnp.bfloat16).reshape(streams * (frames + 1), head_cols)
    attn_part = matmul(attended, lax.all_gather(w_out, "fsdp", axis=1, tiled=True))
    attn_out = (
        lax.psum(attn_part.astype(jnp.bfloat16), "mp")
        .astype(jnp.float32)
        .reshape(streams, frames + 1, width)
    )
    memory_next = jnp.tanh(attn_out[:, frames, :]).astype(jnp.bfloat16)
    hidden_state = inputs.astype(jnp.float32) + attn_out[:, :frames, :]
    h_norm = normalize(hidden_state).astype(jnp.bfloat16).reshape(-1, width)
    halves = lax.all_to_all(h_norm, "fsdp", split_axis=1, concat_axis=0, tiled=True)
    up_sums = lax.psum_scatter(
        matmul(halves, w_up).astype(jnp.bfloat16), "fsdp", scatter_dimension=0, tiled=True
    ).astype(jnp.float32)
    hidden = jax.nn.gelu(up_sums, approximate=True).astype(jnp.bfloat16)
    down_all = matmul(lax.all_gather(hidden, "fsdp", axis=0, tiled=True), w_down)
    down_part = lax.all_to_all(
        down_all.astype(jnp.bfloat16), "fsdp", split_axis=0, concat_axis=1, tiled=True
    ).astype(down_all.dtype)
    down_proj = lax.psum(down_part.astype(jnp.bfloat16), "mp").astype(jnp.float32)
    layer_out = (
        (normalize(hidden_state.reshape(-1, width) + down_proj) * out_gain)
        .astype(jnp.bfloat16)
        .reshape(streams, frames, width)
    )
    center_keys = key_proj[:group_total].reshape(streams, frames, head_cols)[:, :GROUP, :]
    center_values = value_proj[:group_total].reshape(streams, frames, head_cols)[:, :GROUP, :]
    return (layer_out, memory_next, center_keys, center_values)


def solution(mesh):
    in_specs = (
        P(None, ("dp", "fsdp"), None),
        P(("dp", "fsdp"), None, None),
        P(("dp", "fsdp")),
        P(("dp", "fsdp"), None, "mp"),
        P(("dp", "fsdp"), None, "mp"),
        P(("dp", "fsdp")),
        P("fsdp", "mp"),
        P("fsdp", "mp"),
        P("fsdp", "mp"),
        P("mp", "fsdp"),
        P("fsdp", "mp"),
        P("mp", "fsdp"),
        P(),
    )
    out_specs = (
        P(("dp", "fsdp"), None, None),
        P(("dp", "fsdp"), None),
        P(("dp", "fsdp"), None, "mp"),
        P(("dp", "fsdp"), None, "mp"),
    )
    return jax.shard_map(shards, mesh=mesh, in_specs=in_specs, out_specs=out_specs, check_vma=False)
```

profile of v0, /device:TPU:0, one launch (start us, length us, event | category | flops | bytes accessed | tf_op | source)
XLA Modules:
  0.0 236.4 jit_solution(17857175718315085044)
XLA Ops:
  7.2 0.7 all-gather.10.cloned.1.call-update
  8.0 0.7 all-gather.8.cloned.1.call-update
  8.7 0.7 all-gather.6.cloned.1.call-update
  9.4 1.8 copy.120
  11.2 1.4 all_to_all.38
  12.6 8.3 %all-to-all-start = ((bf16[320,16,32]{0,2,1:T(8,128)(2,1)}), bf16[320,16,32]{0,2,1:T(8,128)(2,1)S(1)}, u32[]{:S(2)}, u32[]{:S(2)}) async-start(bf16[320,16,32]{0,2,1:T(8,128)(2,1)} %all_to_all.38), calls=%async_computation | async-start | bytes 786432 | tf_op jit(solution)/shard_map/all_to_all | solution.py:47
  21.6 6.2 %reshape.219 = bf16[32,64,8,64]{3,2,1,0:T(8,128)(2,1)} reshape(bf16[32,64,512]{2,1,0:T(8,128)(2,1)} %param.16) | data formatting | bytes 4194304 | tf_op jit(solution)/shard_map/reshape | solution.py:66
  27.8 6.2 %reshape.221 = bf16[32,64,8,64]{3,2,1,0:T(8,128)(2,1)} reshape(bf16[32,64,512]{2,1,0:T(8,128)(2,1)} %param.17) | data formatting | bytes 4194304 | tf_op jit(solution)/shard_map/reshape | solution.py:67
  34.2 1.7 reshape.233
  35.9 1.8 bitcast_reduce_fusion
  37.9 2.1 multiply_reduce_fusion
  40.1 3.6 %copy.121 = f32[32,5,16,64]{3,2,0,1:T(8,128)} copy(f32[32,5,16,64]{3,1,0,2:T(8,128)} %bitcast.51) | data formatting | bytes 1310720 | tf_op jit(solution)/shard_map/convert_element_type | solution.py:119
  43.7 1.9 copy.122
  45.7 1.8 reshape.230
  48.0 0.9 reshape.216
  49.0 1.7 reshape.231
  50.7 0.9 multiply_convert_fusion.3
  51.6 3.4 %convolution_convert_fusion = bf16[1184,512]{1,0:T(8,128)(2,1)S(1)} fusion(bf16[1024,512]{1,0:T(8,128)(2,1)} %all-gather.10.cloned.1.call-done, bf16[1024,1024]{1,0:T(8,128)(2,1)} %bitcast.57, bf16[160,1024]{1,0:T(8,128)(2,1)} %multiply_convert_fusion.3), kind=kOutput, calls=%fused_computation.4 | convolution fusion | flops 1246969856 | bytes 4685824 | tf_op jit(solution)/shard_map/dot_general | solution.py:21
  55.0 0.7 slice.41
  55.7 1.0 slice.40
  56.7 3.9 %all-gather.8.cloned.1.call-done = bf16[1024,512]{1,0:T(8,128)(2,1)} async-done(((bf16[512,512]{1,0:T(8,128)(2,1)}), bf16[1024,512]{1,0:T(8,128)(2,1)}) %all-gather.8.cloned.1.call-update) | async-done | bytes 1048592 | tf_op jit(solution)/shard_map/all_gather | solution.py:54
  60.6 1.6 convolution_convert_fusion.5
  62.5 1.1 reshape.220
  63.6 3.9 %reshape.218 = bf16[32,32,8,64]{3,2,1,0:T(8,128)(2,1)} reshape(bf16[1024,512]{1,0:T(8,128)(2,1)} %slice.40) | data formatting | bytes 2097152 | tf_op jit(solution)/shard_map/reshape | solution.py:64
  68.1 3.8 %fusion.63 = (f32[32,8,6]{2,1,0:T(8,128)S(1)}, f32[32,8,6,32]{3,2,1,0:T(8,128)S(1)}) fusion(bf16[32,32,8,64]{3,2,1,0:T(8,128)(2,1)} %reshape.218, bf16[32,6,8,64]{3,2,1,0:T(8,128)(2,1)S(1)} %reshape.217, pred[32,6,32]{2,1,0:T(8,128)(4,1)S(1)} %broadcast_and_fusion), kind=kOutput, calls=%fused_computation.93 | convolution fusion | flops 6437376 | bytes 1454080 | tf_op jit(solution)/shard_map/sqhd,skhd->shqk/dot_general | solution.py:77
  71.8 2.4 fusion.64
  74.2 1.0 copy-done.3
  77.0 6.5 %all-gather.6.cloned.1.call-done = bf16[1024,512]{1,0:T(8,128)(2,1)} async-done(((bf16[512,512]{1,0:T(8,128)(2,1)}), bf16[1024,512]{1,0:T(8,128)(2,1)}) %all-gather.6.cloned.1.call-update) | async-done | bytes 1048592 | tf_op jit(solution)/shard_map/all_gather | solution.py:56
  83.5 3.4 %convolution_convert_fusion.1 = bf16[1184,512]{1,0:T(8,128)(2,1)S(1)} fusion(bf16[1024,512]{1,0:T(8,128)(2,1)} %all-gather.6.cloned.1.call-done, bf16[1024,1024]{1,0:T(8,128)(2,1)} %bitcast.58, bf16[160,1024]{1,0:T(8,128)(2,1)} %multiply_convert_fusion.3), kind=kOutput, calls=%fused_computation.5 | convolution fusion | flops 1246969856 | bytes 4685824 | tf_op jit(solution)/shard_map/dot_general | solution.py:21
  86.9 1.0 copy-done.14
  87.9 0.9 reshape.222
  88.9 3.0 %convolution_bitcast_fusion = f32[32,6,8,64]{3,1,2,0:T(8,128)} fusion(f32[32,8,6,5]{2,3,1,0:T(8,128)} %copy-done.6, bf16[32,5,8,64]{3,2,1,0:T(8,128)(2,1)} %reshape.222, f32[32,8,6]{2,1,0:T(8,128)S(1)} %add_add_fusion, f32[32,8,6]{2,1,0:T(8,128)S(1)} %maximum_maximum_fusion), kind=kOutput, calls=%fused_computation.23 | convolution fusion | flops 1006080 | bytes 600064 | tf_op jit(solution)/shard_map/shqk,skhd->sqhd/dot_general | solution.py:108
  91.9 1.0 slice.38
  93.0 3.9 %reshape.215 = bf16[32,32,8,64]{3,2,1,0:T(8,128)(2,1)} reshape(bf16[1024,512]{1,0:T(8,128)(2,1)} %slice.38) | data formatting | bytes 2097152 | tf_op jit(solution)/shard_map/reshape | solution.py:65
  96.9 2.7 %fusion.8 = f32[32,6,8,64]{3,1,2,0:T(8,128)S(1)} fusion(bf16[32,32,8,64]{3,2,1,0:T(8,128)(2,1)} %reshape.215, f32[32,8,6,32]{3,2,1,0:T(8,128)} %copy-done.7, f32[32,8,6]{2,1,0:T(8,128)S(1)} %copy-done.17, f32[32,8,6]{2,1,0:T(8,128)S(1)} %maximum_maximum_fusion), kind=kOutput, calls=%fused_computation.17 | convolution fusion | flops 6438912 | bytes 1650688 | tf_op jit(solution)/shard_map/shqk,skhd->sqhd/dot_general | solution.py:104
  99.7 0.7 copy-done.5
  100.6 1.5 fusion.38
  102.4 3.8 %all-gather.12.cloned.1.call-done = bf16[512,1024]{1,0:T(8,128)(2,1)} async-done(((bf16[512,512]{1,0:T(8,128)(2,1)}), bf16[512,1024]{1,0:T(8,128)(2,1)}) %all-gather.12.cloned.1.call-update) | async-done | bytes 1048592 | tf_op jit(solution)/shard_map/all_gather | solution.py:112
  106.2 2.4 convolution_convert_fusion.3
  108.6 1.1 reshape.224
  109.7 1.0 copy.140
  110.8 18.5 %all-reduce.3.cloned.1.call-done = bf16[32,6,1024]{2,0,1:T(8,128)(2,1)} async-done(((bf16[32,6,1024]{2,0,1:T(8,128)(2,1)}), bf16[32,6,1024]{2,0,1:T(8,128)(2,1)}) %all-reduce.3.cloned.1.call-update) | async-done | bytes 393232 | tf_op jit(solution)/shard_map/psum | solution.py:114
  129.3 1.1 reshape.225
  130.5 0.7 copy-done.8
  131.8 1.0 all_to_all.40
  132.8 1.0 copy.143
  133.8 9.1 %all_to_all.51 = bf16[160,2,512]{2,0,1:T(8,128)(2,1)S(1)} all-to-all(bf16[160,2,512]{2,0,1:T(8,128)(2,1)S(1)} %copy.143), channel_id=1, replica_groups=mesh['dp'=8,'mp'=2,'fsdp'=2] {'fsdp'}, dimensions={1} | all-to-all | bytes 655360 | tf_op jit(solution)/shard_map/all_to_all | solution.py:121
  142.9 2.0 convolution_convert_fusion.2
  145.2 23.3 %reduce-scatter.2.cloned.1.call-done = bf16[160,2048]{1,0:T(8,128)(2,1)} async-done(((bf16[320,2048]{1,0:T(8,128)(2,1)}), bf16[160,2048]{1,0:T(8,128)(2,1)}) %reduce-scatter.2.cloned.1.call-update) | async-done | bytes 655376 | tf_op jit(solution)/shard_map/reduce_scatter | solution.py:122
  168.5 2.4 %fusion.37 = bf16[160,2048]{1,0:T(8,128)(2,1)} fusion(bf16[160,2048]{1,0:T(8,128)(2,1)} %reduce-scatter.2.cloned.1.call-done), kind=kLoop, calls=%fused_computation.32 | loop fusion | flops 3276800 | bytes 1310720 | tf_op jit(solution)/shard_map/convert_element_type | solution.py:125
  171.0 24.3 %all-gather.14.cloned.1.call-done = bf16[320,2048]{1,0:T(8,128)(2,1)} async-done(((bf16[160,2048]{1,0:T(8,128)(2,1)}), bf16[320,2048]{1,0:T(8,128)(2,1)}) %all-gather.14.cloned.1.call-update) | async-done | bytes 1310736 | tf_op jit(solution)/shard_map/all_gather | solution.py:126
  195.3 2.8 %convolution_convert_fusion.4 = bf16[320,512]{1,0:T(8,128)(2,1)S(1)} fusion(bf16[320,2048]{1,0:T(8,128)(2,1)} %all-gather.14.cloned.1.call-done, bf16[2048,512]{1,0:T(8,128)(2,1)} %param.24), kind=kOutput, calls=%fused_computation.35 | convolution fusion | flops 671252480 | bytes 3735552 | tf_op jit(solution)/shard_map/dot_general | solution.py:21
  198.1 8.5 %all_to_all.52 = bf16[2,160,512]{2,1,0:T(8,128)(2,1)S(1)} all-to-all(bf16[2,160,512]{2,1,0:T(8,128)(2,1)S(1)} %bitcast.56), channel_id=1, replica_groups=mesh['dp'=8,'mp'=2,'fsdp'=2] {'fsdp'}, dimensions={0} | all-to-all | bytes 655360 | tf_op jit(solution)/shard_map/all_to_all | solution.py:127
  206.6 0.8 copy.147
  207.5 0.8 reshape.228
  208.3 0.7 slice.46
  209.0 1.7 slice.45
  210.6 1.4 copy.141
  212.0 1.4 reshape.226
  213.4 1.6 fusion.58
  214.9 11.0 %all-reduce.5.cloned.1.call-done = bf16[160,1024]{1,0:T(8,128)(2,1)} async-done(((bf16[160,1024]{1,0:T(8,128)(2,1)}), bf16[160,1024]{1,0:T(8,128)(2,1)}) %all-reduce.5.cloned.1.call-update) | async-done | bytes 327696 | tf_op jit(solution)/shard_map/psum | solution.py:130
  225.9 1.2 fusion.55
  227.1 1.2 multiply_reduce_fusion.1
  228.6 0.9 copy.145
  (96 shorter events, 6.8 us)
Async XLA Ops:
  7.2 135.8 %copy-start = (bf16[512,2048]{1,0:T(8,128)(2,1)S(1)}, bf16[512,2048]{1,0:T(8,128)(2,1)}, u32[]{:S(2)}) copy-start(bf16[512,2048]{1,0:T(8,128)(2,1)} %param.23) | copy-start | bytes 6291460
  7.2 44.4 %all-gather.10.cloned.1.call-start = ((), (), s32[]{:S(2)}) async-start(), calls=%async_computation.6 | async-start | bytes 1572864 | tf_op jit(solution)/shard_map/all_gather | solution.py:55
  7.9 52.7 %all-gather.8.cloned.1.call-start = ((), (), s32[]{:S(2)}) async-start(), calls=%async_computation.5 | async-start | bytes 1572864 | tf_op jit(solution)/shard_map/all_gather | solution.py:54
  8.7 74.8 %all-gather.6.cloned.1.call-start = ((), (), s32[]{:S(2)}) async-start(), calls=%async_computation.4 | async-start | bytes 1572864 | tf_op jit(solution)/shard_map/all_gather | solution.py:56
  9.4 12.1 %copy-start.19 = (s32[32]{0:T(128)S(1)}, s32[32]{0:T(128)}, u32[]{:S(2)}) copy-start(s32[32]{0:T(128)} %param.15) | copy-start | bytes 388
  9.4 12.2 %copy-start.20 = (s32[32]{0:T(128)S(1)}, s32[32]{0:T(128)}, u32[]{:S(2)}) copy-start(s32[32]{0:T(128)} %param.18) | copy-start | bytes 388
  12.6 21.6 %all-to-all-start = ((bf16[320,16,32]{0,2,1:T(8,128)(2,1)}), bf16[320,16,32]{0,2,1:T(8,128)(2,1)S(1)}, u32[]{:S(2)}, u32[]{:S(2)}) async-start(bf16[320,16,32]{0,2,1:T(8,128)(2,1)} %all_to_all.38), calls=%async_computation | async-start | bytes 786432 | tf_op jit(solution)/shard_map/all_to_all | solution.py:47
  20.9 85.3 %all-gather.12.cloned.1.call-start = ((), (), s32[]{:S(2)}) async-start(), calls=%async_computation.7 | async-start | bytes 1572864 | tf_op jit(solution)/shard_map/all_gather | solution.py:112
  21.5 107.8 %all-reduce.3.cloned.1.call-start = ((), (), s32[]{:S(2)}) async-start(), calls=%async_computation.8 | async-start | bytes 786432 | tf_op jit(solution)/shard_map/psum | solution.py:114
  40.1 3.6 %copy-start.1 = (f32[16,5,64,32]{2,1,3,0:T(8,128)S(1)}, f32[16,5,64,32]{2,1,3,0:T(8,128)}, u32[]{:S(2)}) copy-start(f32[16,5,64,32]{2,1,3,0:T(8,128)} %reshape.233) | copy-start | bytes 1966084
  55.0 5.7 %copy-start.10 = (bf16[192,1024]{1,0:T(8,128)(2,1)S(1)}, bf16[192,1024]{1,0:T(8,128)(2,1)}, u32[]{:S(2)}) copy-start(bf16[192,1024]{1,0:T(8,128)(2,1)} %reshape.216) | copy-start | bytes 1179652
  67.5 4.3 %copy-start.2 = (bf16[32,64,8,64]{3,2,1,0:T(8,128)(2,1)S(1)}, bf16[32,64,8,64]{3,2,1,0:T(8,128)(2,1)}, u32[]{:S(2)}) copy-start(bf16[32,64,8,64]{3,2,1,0:T(8,128)(2,1)} %reshape.219) | copy-start | bytes 6291460
  68.0 8.5 %copy-start.6 = (f32[32,8,6,5]{2,3,1,0:T(8,128)}, f32[32,8,6,5]{2,3,1,0:T(8,128)S(1)}, u32[]{:S(2)}) copy-start(f32[32,8,6,5]{2,3,1,0:T(8,128)S(1)} %get-tuple-element.27) | copy-start | bytes 92164
  71.8 4.0 %copy-start.7 = (f32[32,8,6,32]{3,2,1,0:T(8,128)}, f32[32,8,6,32]{3,2,1,0:T(8,128)S(1)}, u32[]{:S(2)}) copy-start(f32[32,8,6,32]{3,2,1,0:T(8,128)S(1)} %get-tuple-element.29) | copy-start | bytes 589828
  74.2 1.0 copy-start.3
  86.9 1.0 copy-start.14
  87.9 4.0 %copy-start.12 = (bf16[160,512]{1,0:T(8,128)(2,1)}, bf16[160,512]{1,0:T(8,128)(2,1)S(1)}, u32[]{:S(2)}) copy-start(bf16[160,512]{1,0:T(8,128)(2,1)S(1)} %slice.42) | copy-start | bytes 491524
  88.9 3.0 %copy-start.16 = (f32[32,8,6]{2,1,0:T(8,128)}, f32[32,8,6]{2,1,0:T(8,128)S(1)}, u32[]{:S(2)}) copy-start(f32[32,8,6]{2,1,0:T(8,128)S(1)} %add_add_fusion) | copy-start | bytes 18436
  88.9 3.0 %copy-start.15 = (bf16[1184,512]{1,0:T(8,128)(2,1)S(1)}, bf16[1184,512]{1,0:T(8,128)(2,1)}, u32[]{:S(2)}) copy-start(bf16[1184,512]{1,0:T(8,128)(2,1)} %copy-done.14) | copy-start | bytes 3637252
  93.0 3.9 %copy-start.17 = (f32[32,8,6]{2,1,0:T(8,128)S(1)}, f32[32,8,6]{2,1,0:T(8,128)}, u32[]{:S(2)}) copy-start(f32[32,8,6]{2,1,0:T(8,128)} %copy-done.16) | copy-start | bytes 18436
  96.9 2.8 %copy-start.4 = (f32[32,8,6,64]{3,2,1,0:T(8,128)S(1)}, f32[32,8,6,64]{3,2,1,0:T(8,128)}, u32[]{:S(2)}) copy-start(f32[32,8,6,64]{3,2,1,0:T(8,128)} %copy-done.3) | copy-start | bytes 1179652
  96.9 3.5 %copy-start.5 = (bf16[32,64,8,64]{3,2,1,0:T(8,128)(2,1)S(1)}, bf16[32,64,8,64]{3,2,1,0:T(8,128)(2,1)}, u32[]{:S(2)}) copy-start(bf16[32,64,8,64]{3,2,1,0:T(8,128)(2,1)} %reshape.221) | copy-start | bytes 6291460
  96.9 3.7 %copy-start.21 = (f32[32,6,8,64]{3,1,2,0:T(8,128)S(1)}, f32[32,6,8,64]{3,1,2,0:T(8,128)}, u32[]{:S(2)}) copy-start(f32[32,6,8,64]{3,1,2,0:T(8,128)} %convolution_bitcast_fusion) | copy-start | bytes 1179652
  110.7 57.8 %reduce-scatter.2.cloned.1.call-start = ((), (), s32[]{:S(2)}) async-start(), calls=%async_computation.9 | async-start | bytes 1966080 | tf_op jit(solution)/shard_map/reduce_scatter | solution.py:122
  130.3 0.9 copy-start.8
  144.9 50.4 %all-gather.14.cloned.1.call-start = ((), (), s32[]{:S(2)}) async-start(), calls=%async_computation.10 | async-start | bytes 1966080 | tf_op jit(solution)/shard_map/all_gather | solution.py:126
  170.9 36.5 %copy-start.13 = (bf16[160,512]{1,0:T(8,128)(2,1)S(1)}, bf16[160,512]{1,0:T(8,128)(2,1)}, u32[]{:S(2)}) copy-start(bf16[160,512]{1,0:T(8,128)(2,1)} %copy-done.12) | copy-start | bytes 491524
  170.9 55.0 %all-reduce.5.cloned.1.call-start = ((), (), s32[]{:S(2)}) async-start(), calls=%async_computation.11 | async-start | bytes 655360 | tf_op jit(solution)/shard_map/psum | solution.py:130
  198.1 9.4 %copy-start.11 = (bf16[160,512]{1,0:T(8,128)(2,1)S(1)}, bf16[160,512]{1,0:T(8,128)(2,1)}, u32[]{:S(2)}) copy-start(bf16[160,512]{1,0:T(8,128)(2,1)} %slice.41) | copy-start | bytes 491524
  212.0 16.3 %copy-start.18 = (f32[1024]{0:T(1024)S(1)}, f32[1024]{0:T(1024)}, u32[]{:S(2)}) copy-start(f32[1024]{0:T(1024)} %param.25) | copy-start | bytes 12292
  225.9 2.4 %copy-start.9 = (bf16[160,1024]{1,0:T(8,128)(2,1)S(1)}, bf16[160,1024]{1,0:T(8,128)(2,1)}, u32[]{:S(2)}) copy-start(bf16[160,1024]{1,0:T(8,128)(2,1)} %all-reduce.5.cloned.1.call-done) | copy-start | bytes 983044
Sparse Core Ops, SparseCore 0:
  9.5 28.2 all-gather.9
  39.3 21.2 all-gather.7
  62.2 21.2 all-gather.5
  84.9 21.2 all-gather.11
  110.8 18.3 all-reduce.2
  145.0 23.4 reduce-scatter.1
  171.0 24.2 all-gather.13
  207.5 18.3 all-reduce.4
where the time goes:
time: 238 us; the launch traced here: 236 us
  waiting for transfers between devices  94 us (39%)
  local copies, waits for them, and re-layouts  56.7 us (24%)
  matrix products  29.4 us (12%)
  blocking collectives  17.6 us (7%)
  other arithmetic  15.2 us (6%)
  between operations  14.6 us (6%)
  starting transfers between devices  8.88 us (4%)
    all_gather x1, waiting for transfers between devices, shards(): lax.all_gather(hidden, 'fsdp', axis=0, tiled=True)  24.3 us
    reduce_scatter x1, waiting for transfers between devices, shards(): lax.psum_scatter(matmul(halves, w_up).astype(jnp.bfloat16), 'fsdp', scatt...  23.3 us
    psum x1, waiting for transfers between devices, shards(): lax.psum(attn_part.astype(jnp.bfloat16), 'mp').astype(jnp.float32)  18.5 us
    dot_general x6, matrix products, matmul(): return jnp.dot(left, right, preferred_element_type=jnp.float32)  15.5 us
    psum x1, waiting for transfers between devices, shards(): lax.psum(down_part.astype(jnp.bfloat16), 'mp').astype(jnp.float32)  11 us
    convert_element_type x5, local copies, waits for them, and re-layouts, shards(): hidden_state = inputs.astype(jnp.float32) + attn_out[:, :frames, :]  10.6 us
    all_to_all x1, blocking collectives, shards(): lax.all_to_all(h_norm, 'fsdp', split_axis=1, concat_axis=0, tiled=True)  9.13 us
    all_to_all x1, blocking collectives, shards(): lax.all_to_all(down_all.astype(jnp.bfloat16), 'fsdp', split_axis=0, conca...  8.51 us
  transfers between devices with their start and end apart: 9, of which 7 were waited for; matrix products, arithmetic and copies ran while one was open for 32% of the time, Pallas kernels for 0%

commit v1 on v0

--- a/solution.py
+++ b/solution.py
@@ -123,7 +123,12 @@
         matmul(halves, w_up).astype(jnp.bfloat16), "fsdp", scatter_dimension=0, tiled=True
     ).astype(jnp.float32)
     hidden = jax.nn.gelu(up_sums, approximate=True).astype(jnp.bfloat16)
-    down_all = matmul(lax.all_gather(hidden, "fsdp", axis=0, tiled=True), w_down)
+    down_all = matmul(
+        jnp.concatenate(
+            lax.all_to_all(jnp.stack([hidden] * lax.axis_size("fsdp")), "fsdp", 0, 0), axis=0
+        ),
+        w_down,
+    )
     down_part = lax.all_to_all(
         down_all.astype(jnp.bfloat16), "fsdp", split_axis=0, concat_axis=1, tiled=True
     ).astype(down_all.dtype)

time: 238 us -> 229 us (0.962)
  waiting for transfers between devices: 94 us -> 69.7 us
  blocking collectives: 17.6 us -> 36.3 us
    all_gather x1 -> x0, waiting for transfers between devices: 24.3 us -> none  [shards(): lax.all_gather(hidden, 'fsdp', axis=0, tiled=True)]
    all_to_all x0 -> x1, blocking collectives: none -> 19.1 us  [shards(): lax.all_to_all(jnp.stack([hidden] * lax.axis_size('fsdp')), 'fsdp', 0, 0)]
    unnamed x46 -> x48, local copies, waits for them, and re-layouts: 6.48 us -> 6.51 us
  transfers between devices with their start and end apart: 9 -> 8, of which waited for: 7 -> 6; matrix products, arithmetic and copies ran while one was open for 32% -> 34% of each run, Pallas kernels for 0% -> 0%
where the time goes in v1:
time: 229 us; the launch traced here: 228 us
  waiting for transfers between devices  69.7 us (30%)
  local copies, waits for them, and re-layouts  56.7 us (25%)
  blocking collectives  36.3 us (16%)
  matrix products  27.4 us (12%)
  between operations  14.6 us (6%)
  other arithmetic  14.5 us (6%)
  starting transfers between devices  8.84 us (4%)
    reduce_scatter x1, waiting for transfers between devices, shards(): lax.psum_scatter(matmul(halves, w_up).astype(jnp.bfloat16), 'fsdp', scatt...  23.3 us
    all_to_all x1, blocking collectives, shards(): lax.all_to_all(jnp.stack([hidden] * lax.axis_size('fsdp')), 'fsdp', 0, 0)  19.1 us
    psum x1, waiting for transfers between devices, shards(): lax.psum(attn_part.astype(jnp.bfloat16), 'mp').astype(jnp.float32)  18.5 us
    dot_general x6, matrix products, matmul(): return jnp.dot(left, right, preferred_element_type=jnp.float32)  13.5 us
    psum x1, waiting for transfers between devices, shards(): lax.psum(down_part.astype(jnp.bfloat16), 'mp').astype(jnp.float32)  11 us
    convert_element_type x5, local copies, waits for them, and re-layouts, shards(): hidden_state = inputs.astype(jnp.float32) + attn_out[:, :frames, :]  10.6 us
    all_to_all x1, blocking collectives, shards(): lax.all_to_all(h_norm, 'fsdp', split_axis=1, concat_axis=0, tiled=True)  9.13 us
    all_to_all x1, starting transfers between devices, shards(): lax.all_to_all(flattened, ('dp', 'fsdp'), split_axis=1, concat_axis=0, ti...  8.34 us
  transfers between devices with their start and end apart: 8, of which 6 were waited for; matrix products, arithmetic and copies ran while one was open for 34% of the time, Pallas kernels for 0%

profile of v1, /device:TPU:0, one launch (start us, length us, event | category | flops | bytes accessed | tf_op | source)
XLA Modules:
  0.0 228.0 jit_solution(16473094840022437714)
XLA Ops:
  7.2 0.7 all-gather.9.cloned.1.call-update
  8.0 0.7 all-gather.7.cloned.1.call-update
  8.7 0.7 all-gather.5.cloned.1.call-update
  9.4 1.8 copy.120
  11.2 1.4 all_to_all.41
  12.6 8.3 %all-to-all-start = ((bf16[320,16,32]{0,2,1:T(8,128)(2,1)}), bf16[320,16,32]{0,2,1:T(8,128)(2,1)S(1)}, u32[]{:S(2)}, u32[]{:S(2)}) async-start(bf16[320,16,32]{0,2,1:T(8,128)(2,1)} %all_to_all.41), calls=%async_computation | async-start | bytes 786432 | tf_op jit(solution)/shard_map/all_to_all | solution.py:47
  21.6 6.2 %reshape.222 = bf16[32,64,8,64]{3,2,1,0:T(8,128)(2,1)} reshape(bf16[32,64,512]{2,1,0:T(8,128)(2,1)} %param.16) | data formatting | bytes 4194304 | tf_op jit(solution)/shard_map/reshape | solution.py:66
  27.8 6.1 %reshape.224 = bf16[32,64,8,64]{3,2,1,0:T(8,128)(2,1)} reshape(bf16[32,64,512]{2,1,0:T(8,128)(2,1)} %param.17) | data formatting | bytes 4194304 | tf_op jit(solution)/shard_map/reshape | solution.py:67
  34.2 1.7 reshape.237
  35.9 1.8 bitcast_reduce_fusion
  37.9 2.1 multiply_reduce_fusion
  40.1 3.6 %copy.121 = f32[32,5,16,64]{3,2,0,1:T(8,128)} copy(f32[32,5,16,64]{3,1,0,2:T(8,128)} %bitcast.54) | data formatting | bytes 1310720 | tf_op jit(solution)/shard_map/convert_element_type | solution.py:119
  43.7 1.9 copy.122
  45.7 1.8 reshape.234
  48.0 0.9 reshape.219
  49.0 1.7 reshape.235
  50.7 0.9 multiply_convert_fusion.3
  51.6 3.4 %convolution_convert_fusion = bf16[1184,512]{1,0:T(8,128)(2,1)S(1)} fusion(bf16[1024,512]{1,0:T(8,128)(2,1)} %all-gather.9.cloned.1.call-done, bf16[1024,1024]{1,0:T(8,128)(2,1)} %bitcast.61, bf16[160,1024]{1,0:T(8,128)(2,1)} %multiply_convert_fusion.3), kind=kOutput, calls=%fused_computation.4 | convolution fusion | flops 1246969856 | bytes 4685824 | tf_op jit(solution)/shard_map/dot_general | solution.py:21
  55.0 0.7 slice.41
  55.6 1.0 slice.40
  56.7 4.0 %all-gather.7.cloned.1.call-done = bf16[1024,512]{1,0:T(8,128)(2,1)} async-done(((bf16[512,512]{1,0:T(8,128)(2,1)}), bf16[1024,512]{1,0:T(8,128)(2,1)}) %all-gather.7.cloned.1.call-update) | async-done | bytes 1048592 | tf_op jit(solution)/shard_map/all_gather | solution.py:54
  60.6 1.6 convolution_convert_fusion.5
  62.5 1.1 reshape.223
  63.6 3.9 %reshape.221 = bf16[32,32,8,64]{3,2,1,0:T(8,128)(2,1)} reshape(bf16[1024,512]{1,0:T(8,128)(2,1)} %slice.40) | data formatting | bytes 2097152 | tf_op jit(solution)/shard_map/reshape | solution.py:64
  68.1 3.8 %fusion.64 = (f32[32,8,6]{2,1,0:T(8,128)S(1)}, f32[32,8,6,32]{3,2,1,0:T(8,128)S(1)}) fusion(bf16[32,32,8,64]{3,2,1,0:T(8,128)(2,1)} %reshape.221, bf16[32,6,8,64]{3,2,1,0:T(8,128)(2,1)S(1)} %reshape.220, pred[32,6,32]{2,1,0:T(8,128)(4,1)S(1)} %broadcast_and_fusion), kind=kOutput, calls=%fused_computation.95 | convolution fusion | flops 6437376 | bytes 1454080 | tf_op jit(solution)/shard_map/sqhd,skhd->shqk/dot_general | solution.py:77
  71.8 2.4 %fusion.65 = (f32[32,8,6]{2,1,0:T(8,128)S(1)}, f32[32,8,6,64]{3,2,1,0:T(8,128)S(1)}) fusion(bf16[32,64,8,64]{3,2,1,0:T(8,128)(2,1)S(1)} %copy-done.2, bf16[32,6,8,64]{3,2,1,0:T(8,128)(2,1)S(1)} %reshape.220, pred[32,64]{1,0:T(8,128)(4,1)S(1)} %iota_compare_fusion), kind=kOutput, calls=%fused_computation.96 | convolution fusion | flops 12876288 | bytes 2695168 | tf_op jit(solution)/shard_map/sqhd,skhd->shqk/dot_general | solution.py:80
  74.2 1.0 copy-done.3
  77.0 6.5 %all-gather.5.cloned.1.call-done = bf16[1024,512]{1,0:T(8,128)(2,1)} async-done(((bf16[512,512]{1,0:T(8,128)(2,1)}), bf16[1024,512]{1,0:T(8,128)(2,1)}) %all-gather.5.cloned.1.call-update) | async-done | bytes 1048592 | tf_op jit(solution)/shard_map/all_gather | solution.py:56
  83.5 3.4 %convolution_convert_fusion.1 = bf16[1184,512]{1,0:T(8,128)(2,1)S(1)} fusion(bf16[1024,512]{1,0:T(8,128)(2,1)} %all-gather.5.cloned.1.call-done, bf16[1024,1024]{1,0:T(8,128)(2,1)} %bitcast.62, bf16[160,1024]{1,0:T(8,128)(2,1)} %multiply_convert_fusion.3), kind=kOutput, calls=%fused_computation.5 | convolution fusion | flops 1246969856 | bytes 4685824 | tf_op jit(solution)/shard_map/dot_general | solution.py:21
  86.9 1.0 copy-done.14
  87.9 0.9 reshape.225
  88.9 3.0 %convolution_bitcast_fusion = f32[32,6,8,64]{3,1,2,0:T(8,128)} fusion(f32[32,8,6,5]{2,3,1,0:T(8,128)} %copy-done.6, bf16[32,5,8,64]{3,2,1,0:T(8,128)(2,1)} %reshape.225, f32[32,8,6]{2,1,0:T(8,128)S(1)} %add_add_fusion, f32[32,8,6]{2,1,0:T(8,128)S(1)} %maximum_maximum_fusion), kind=kOutput, calls=%fused_computation.23 | convolution fusion | flops 1006080 | bytes 600064 | tf_op jit(solution)/shard_map/shqk,skhd->sqhd/dot_general | solution.py:108
  92.0 1.0 slice.38
  93.0 3.9 %reshape.218 = bf16[32,32,8,64]{3,2,1,0:T(8,128)(2,1)} reshape(bf16[1024,512]{1,0:T(8,128)(2,1)} %slice.38) | data formatting | bytes 2097152 | tf_op jit(solution)/shard_map/reshape | solution.py:65
  96.9 2.7 %fusion.8 = f32[32,6,8,64]{3,1,2,0:T(8,128)S(1)} fusion(bf16[32,32,8,64]{3,2,1,0:T(8,128)(2,1)} %reshape.218, f32[32,8,6,32]{3,2,1,0:T(8,128)} %copy-done.7, f32[32,8,6]{2,1,0:T(8,128)S(1)} %copy-done.17, f32[32,8,6]{2,1,0:T(8,128)S(1)} %maximum_maximum_fusion), kind=kOutput, calls=%fused_computation.17 | convolution fusion | flops 6438912 | bytes 1650688 | tf_op jit(solution)/shard_map/shqk,skhd->sqhd/dot_general | solution.py:104
  99.7 0.7 copy-done.5
  100.6 1.5 fusion.38
  102.4 3.8 %all-gather.11.cloned.1.call-done = bf16[512,1024]{1,0:T(8,128)(2,1)} async-done(((bf16[512,512]{1,0:T(8,128)(2,1)}), bf16[512,1024]{1,0:T(8,128)(2,1)}) %all-gather.11.cloned.1.call-update) | async-done | bytes 1048592 | tf_op jit(solution)/shard_map/all_gather | solution.py:112
  106.2 2.4 %convolution_convert_fusion.3 = bf16[192,1024]{1,0:T(8,128)(2,1)} fusion(bf16[192,512]{1,0:T(8,128)(2,1)S(1)} %reshape.226, bf16[512,1024]{1,0:T(8,128)(2,1)} %all-gather.11.cloned.1.call-done), kind=kOutput, calls=%fused_computation.35 | convolution fusion | flops 201523200 | bytes 1638400 | tf_op jit(solution)/shard_map/dot_general | solution.py:21
  108.6 1.1 reshape.227
  109.7 1.0 copy.140
  110.8 18.5 %all-reduce.3.cloned.1.call-done = bf16[32,6,1024]{2,0,1:T(8,128)(2,1)} async-done(((bf16[32,6,1024]{2,0,1:T(8,128)(2,1)}), bf16[32,6,1024]{2,0,1:T(8,128)(2,1)}) %all-reduce.3.cloned.1.call-update) | async-done | bytes 393232 | tf_op jit(solution)/shard_map/psum | solution.py:114
  129.3 1.1 reshape.228
  130.5 0.8 copy-done.8
  131.9 1.0 all_to_all.43
  132.8 1.0 copy.143
  133.8 9.1 %all_to_all.56 = bf16[160,2,512]{2,0,1:T(8,128)(2,1)S(1)} all-to-all(bf16[160,2,512]{2,0,1:T(8,128)(2,1)S(1)} %copy.143), channel_id=1, replica_groups=mesh['dp'=8,'mp'=2,'fsdp'=2] {'fsdp'}, dimensions={1} | all-to-all | bytes 655360 | tf_op jit(solution)/shard_map/all_to_all | solution.py:121
  143.0 1.9 convolution_convert_fusion.2
  145.2 23.3 %reduce-scatter.2.cloned.1.call-done = bf16[160,2048]{1,0:T(8,128)(2,1)} async-done(((bf16[320,2048]{1,0:T(8,128)(2,1)}), bf16[160,2048]{1,0:T(8,128)(2,1)}) %reduce-scatter.2.cloned.1.call-update) | async-done | bytes 655376 | tf_op jit(solution)/shard_map/reduce_scatter | solution.py:122
  168.5 1.5 fusion.44
  170.2 19.1 %all_to_all.57 = bf16[2,160,2048]{2,1,0:T(8,128)(2,1)S(1)} all-to-all(bf16[2,160,2048]{2,1,0:T(8,128)(2,1)S(1)} %pad_maximum_fusion.3), channel_id=1, replica_groups=mesh['dp'=8,'mp'=2,'fsdp'=2] {'fsdp'}, dimensions={0} | all-to-all | bytes 2621440 | tf_op jit(solution)/shard_map/all_to_all | solution.py:128
  189.3 0.9 convolution_convert_fusion.4
  190.2 8.1 %all_to_all.58 = bf16[2,160,512]{2,1,0:T(8,128)(2,1)S(1)} all-to-all(bf16[2,160,512]{2,1,0:T(8,128)(2,1)S(1)} %bitcast.60), channel_id=1, replica_groups=mesh['dp'=8,'mp'=2,'fsdp'=2] {'fsdp'}, dimensions={0} | all-to-all | bytes 655360 | tf_op jit(solution)/shard_map/all_to_all | solution.py:132
  198.3 0.8 copy.147
  199.1 0.8 reshape.232
  199.9 0.7 slice.46
  200.6 1.7 slice.45
  202.3 1.4 copy.141
  203.6 1.4 reshape.229
  205.0 1.6 fusion.59
  206.6 11.0 %all-reduce.5.cloned.1.call-done = bf16[160,1024]{1,0:T(8,128)(2,1)} async-done(((bf16[160,1024]{1,0:T(8,128)(2,1)}), bf16[160,1024]{1,0:T(8,128)(2,1)}) %all-reduce.5.cloned.1.call-update) | async-done | bytes 327696 | tf_op jit(solution)/shard_map/psum | solution.py:135
  217.5 1.2 fusion.56
  218.7 1.2 multiply_reduce_fusion.1
  220.3 0.9 copy.145
  (97 shorter events, 6.9 us)
Async XLA Ops:
  7.2 135.8 %copy-start = (bf16[512,2048]{1,0:T(8,128)(2,1)S(1)}, bf16[512,2048]{1,0:T(8,128)(2,1)}, u32[]{:S(2)}) copy-start(bf16[512,2048]{1,0:T(8,128)(2,1)} %param.23) | copy-start | bytes 6291460
  7.2 44.4 %all-gather.9.cloned.1.call-start = ((), (), s32[]{:S(2)}) async-start(), calls=%async_computation.7 | async-start | bytes 1572864 | tf_op jit(solution)/shard_map/all_gather | solution.py:55
  7.9 52.7 %all-gather.7.cloned.1.call-start = ((), (), s32[]{:S(2)}) async-start(), calls=%async_computation.6 | async-start | bytes 1572864 | tf_op jit(solution)/shard_map/all_gather | solution.py:54
  8.7 74.8 %all-gather.5.cloned.1.call-start = ((), (), s32[]{:S(2)}) async-start(), calls=%async_computation.5 | async-start | bytes 1572864 | tf_op jit(solution)/shard_map/all_gather | solution.py:56
  9.4 12.1 %copy-start.20 = (s32[32]{0:T(128)S(1)}, s32[32]{0:T(128)}, u32[]{:S(2)}) copy-start(s32[32]{0:T(128)} %param.15) | copy-start | bytes 388
  9.4 12.2 %copy-start.21 = (s32[32]{0:T(128)S(1)}, s32[32]{0:T(128)}, u32[]{:S(2)}) copy-start(s32[32]{0:T(128)} %param.18) | copy-start | bytes 388
  12.6 21.6 %all-to-all-start = ((bf16[320,16,32]{0,2,1:T(8,128)(2,1)}), bf16[320,16,32]{0,2,1:T(8,128)(2,1)S(1)}, u32[]{:S(2)}, u32[]{:S(2)}) async-start(bf16[320,16,32]{0,2,1:T(8,128)(2,1)} %all_to_all.41), calls=%async_computation | async-start | bytes 786432 | tf_op jit(solution)/shard_map/all_to_all | solution.py:47
  20.9 85.3 %all-gather.11.cloned.1.call-start = ((), (), s32[]{:S(2)}) async-start(), calls=%async_computation.8 | async-start | bytes 1572864 | tf_op jit(solution)/shard_map/all_gather | solution.py:112
  21.5 107.8 %all-reduce.3.cloned.1.call-start = ((), (), s32[]{:S(2)}) async-start(), calls=%async_computation.9 | async-start | bytes 786432 | tf_op jit(solution)/shard_map/psum | solution.py:114
  40.1 3.6 %copy-start.1 = (f32[16,5,64,32]{2,1,3,0:T(8,128)S(1)}, f32[16,5,64,32]{2,1,3,0:T(8,128)}, u32[]{:S(2)}) copy-start(f32[16,5,64,32]{2,1,3,0:T(8,128)} %reshape.237) | copy-start | bytes 1966084
  55.0 5.7 %copy-start.10 = (bf16[192,1024]{1,0:T(8,128)(2,1)S(1)}, bf16[192,1024]{1,0:T(8,128)(2,1)}, u32[]{:S(2)}) copy-start(bf16[192,1024]{1,0:T(8,128)(2,1)} %reshape.219) | copy-start | bytes 1179652
  67.5 4.3 %copy-start.2 = (bf16[32,64,8,64]{3,2,1,0:T(8,128)(2,1)S(1)}, bf16[32,64,8,64]{3,2,1,0:T(8,128)(2,1)}, u32[]{:S(2)}) copy-start(bf16[32,64,8,64]{3,2,1,0:T(8,128)(2,1)} %reshape.222) | copy-start | bytes 6291460
  68.0 8.5 %copy-start.6 = (f32[32,8,6,5]{2,3,1,0:T(8,128)}, f32[32,8,6,5]{2,3,1,0:T(8,128)S(1)}, u32[]{:S(2)}) copy-start(f32[32,8,6,5]{2,3,1,0:T(8,128)S(1)} %get-tuple-element.27) | copy-start | bytes 92164
  71.8 4.0 %copy-start.7 = (f32[32,8,6,32]{3,2,1,0:T(8,128)}, f32[32,8,6,32]{3,2,1,0:T(8,128)S(1)}, u32[]{:S(2)}) copy-start(f32[32,8,6,32]{3,2,1,0:T(8,128)S(1)} %get-tuple-element.29) | copy-start | bytes 589828
  74.2 1.0 copy-start.3
  86.9 1.0 copy-start.14
  87.9 4.0 %copy-start.12 = (bf16[160,512]{1,0:T(8,128)(2,1)}, bf16[160,512]{1,0:T(8,128)(2,1)S(1)}, u32[]{:S(2)}) copy-start(bf16[160,512]{1,0:T(8,128)(2,1)S(1)} %slice.42) | copy-start | bytes 491524
  88.9 3.0 %copy-start.16 = (f32[32,8,6]{2,1,0:T(8,128)}, f32[32,8,6]{2,1,0:T(8,128)S(1)}, u32[]{:S(2)}) copy-start(f32[32,8,6]{2,1,0:T(8,128)S(1)} %add_add_fusion) | copy-start | bytes 18436
  88.9 3.0 %copy-start.15 = (bf16[1184,512]{1,0:T(8,128)(2,1)S(1)}, bf16[1184,512]{1,0:T(8,128)(2,1)}, u32[]{:S(2)}) copy-start(bf16[1184,512]{1,0:T(8,128)(2,1)} %copy-done.14) | copy-start | bytes 3637252
  93.0 3.9 %copy-start.17 = (f32[32,8,6]{2,1,0:T(8,128)S(1)}, f32[32,8,6]{2,1,0:T(8,128)}, u32[]{:S(2)}) copy-start(f32[32,8,6]{2,1,0:T(8,128)} %copy-done.16) | copy-start | bytes 18436
  96.9 2.8 %copy-start.4 = (f32[32,8,6,64]{3,2,1,0:T(8,128)S(1)}, f32[32,8,6,64]{3,2,1,0:T(8,128)}, u32[]{:S(2)}) copy-start(f32[32,8,6,64]{3,2,1,0:T(8,128)} %copy-done.3) | copy-start | bytes 1179652
  96.9 3.5 %copy-start.5 = (bf16[32,64,8,64]{3,2,1,0:T(8,128)(2,1)S(1)}, bf16[32,64,8,64]{3,2,1,0:T(8,128)(2,1)}, u32[]{:S(2)}) copy-start(bf16[32,64,8,64]{3,2,1,0:T(8,128)(2,1)} %reshape.224) | copy-start | bytes 6291460
  96.9 3.7 %copy-start.22 = (f32[32,6,8,64]{3,1,2,0:T(8,128)S(1)}, f32[32,6,8,64]{3,1,2,0:T(8,128)}, u32[]{:S(2)}) copy-start(f32[32,6,8,64]{3,1,2,0:T(8,128)} %convolution_bitcast_fusion) | copy-start | bytes 1179652
  110.7 57.8 %reduce-scatter.2.cloned.1.call-start = ((), (), s32[]{:S(2)}) async-start(), calls=%async_computation.10 | async-start | bytes 1966080 | tf_op jit(solution)/shard_map/reduce_scatter | solution.py:122
  130.3 0.9 copy-start.8
  144.9 72.6 %all-reduce.5.cloned.1.call-start = ((), (), s32[]{:S(2)}) async-start(), calls=%async_computation.11 | async-start | bytes 655360 | tf_op jit(solution)/shard_map/psum | solution.py:135
  170.1 19.3 %copy-start.19 = (bf16[2048,512]{1,0:T(8,128)(2,1)S(1)}, bf16[2048,512]{1,0:T(8,128)(2,1)}, u32[]{:S(2)}) copy-start(bf16[2048,512]{1,0:T(8,128)(2,1)} %param.24) | copy-start | bytes 6291460
  189.3 9.7 %copy-start.13 = (bf16[160,512]{1,0:T(8,128)(2,1)S(1)}, bf16[160,512]{1,0:T(8,128)(2,1)}, u32[]{:S(2)}) copy-start(bf16[160,512]{1,0:T(8,128)(2,1)} %copy-done.12) | copy-start | bytes 491524
  190.2 8.9 %copy-start.11 = (bf16[160,512]{1,0:T(8,128)(2,1)S(1)}, bf16[160,512]{1,0:T(8,128)(2,1)}, u32[]{:S(2)}) copy-start(bf16[160,512]{1,0:T(8,128)(2,1)} %slice.41) | copy-start | bytes 491524
  203.6 16.3 %copy-start.18 = (f32[1024]{0:T(1024)S(1)}, f32[1024]{0:T(1024)}, u32[]{:S(2)}) copy-start(f32[1024]{0:T(1024)} %param.25) | copy-start | bytes 12292
  217.5 2.4 %copy-start.9 = (bf16[160,1024]{1,0:T(8,128)(2,1)S(1)}, bf16[160,1024]{1,0:T(8,128)(2,1)}, u32[]{:S(2)}) copy-start(bf16[160,1024]{1,0:T(8,128)(2,1)} %all-reduce.5.cloned.1.call-done) | copy-start | bytes 983044
Sparse Core Ops, SparseCore 0:
  9.5 28.2 all-gather.8
  39.3 21.2 all-gather.6
  62.2 21.2 all-gather.4
  84.9 21.2 all-gather.10
  110.8 18.3 all-reduce.2
  145.1 23.4 reduce-scatter.1
  199.2 18.3 all-reduce.4
